TPU v7x, 32 devices: a whole 2x2x4 slice. The times are simulated.
32 devices in a mesh: section: 4 (over y, core), dp: 8 (over z, x).
Axes of the slice: x: 2, y: 2, z: 4, core: 2. Of those that a mesh axis runs over, the one named last changes fastest.
Arguments:
- section_inputs: bfloat16 [4, 2, 1024, 1024], P('section', None, 'dp'), may hold values from -6 to 6
- gain: float32 [4, 1024], P('section'), may hold values from 0.25 to 1.75
- w_gate: bfloat16 [4, 1024, 1536], P('section'), may hold values from -0.1875 to 0.1875
- w_up: bfloat16 [4, 1024, 1536], P('section'), may hold values from -0.1875 to 0.1875
- w_out: bfloat16 [4, 1024, 1536], P('section'), may hold values from -0.15625 to 0.15625
- out_grad: bfloat16 [2, 1024, 1024], P(None, 'dp'), may hold values from -6 to 6
Outputs:
- grad_w_gate: float32 [4, 1024, 1536], P('section', 'dp')
- grad_w_up: float32 [4, 1024, 1536], P('section', 'dp')
- grad_w_out: float32 [4, 1024, 1536], P('section', 'dp')
- grad_gain: float32 [4, 1024], P('section', 'dp')
- input_grads: bfloat16 [4, 2, 1024, 1024], P('section', None, 'dp')
All inputs are finite; a program needn't handle non-finite values.
Results may differ from a plain program's by a relative error of at most 0.014.
Values may be sent and summed in bfloat16 or wider, within the bound.
A program may use at most 128 MiB of HBM per device.

v0:
```python
import jax
import jax.numpy as jnp
from jax import lax
from jax.sharding import PartitionSpec as P

C_GELU = 0.7978845608028654
EPSILON = 1e-06


def from_behind(value, axis, steps):
    count = lax.axis_size(axis)
    leading, last = (max(0, -steps), min(count, count - steps))
    return lax.ppermute(value, axis, [(source, source + steps) for source in range(leading, last)])


def gelu_parts(pre_act):
    cubic = 0.044715 * pre_act * pre_act * pre_act
    tangent = jnp.tanh(C_GELU * (pre_act + cubic))
    gelu_value = 0.5 * pre_act * (1.0 + tangent)
    gelu_slope = 0.5 * (1.0 + tangent) + 0.5 * pre_act * (1.0 - tangent * tangent) * C_GELU * (
        1.0 + 3.0 * 0.044715 * pre_act * pre_act
    )
    return (gelu_value, gelu_slope)


def section_back(inputs_row, incoming, gain_row, w_gate_mat, w_up_mat, w_out_mat):
    inputs_float = inputs_row.astype(jnp.float32)
    inverse_rms = lax.rsqrt(jnp.mean(inputs_float * inputs_float, axis=-1, keepdims=True) + EPSILON)
    normed = (inputs_float * inverse_rms * gain_row).astype(jnp.bfloat16)
    gate_pre = jnp.dot(normed, w_gate_mat, preferred_element_type=jnp.float32)
    up_pre = jnp.dot(normed, w_up_mat, preferred_element_type=jnp.float32)
    gelu_value, gelu_slope = gelu_parts(gate_pre)
    hidden_act = (gelu_value * up_pre).astype(jnp.bfloat16)
    act_grad = jnp.dot(incoming, w_out_mat, preferred_element_type=jnp.float32)
    gate_grad = (act_grad * up_pre * gelu_slope).astype(jnp.bfloat16)
    up_grad = (act_grad * gelu_value).astype(jnp.bfloat16)
    transpose_dims = (((1,), (1,)), ((), ()))
    normed_grad = lax.dot_general(
        gate_grad, w_gate_mat, transpose_dims, preferred_element_type=jnp.float32
    )
    normed_grad = normed_grad + lax.dot_general(
        up_grad, w_up_mat, transpose_dims, preferred_element_type=jnp.float32
    )
    gain_term = jnp.sum(normed_grad * inputs_float * inverse_rms, axis=0)
    scaled_grad = normed_grad * gain_row
    input_grad = inverse_rms * scaled_grad - inputs_float * inverse_rms**3 * jnp.mean(
        scaled_grad * inputs_float, axis=-1, keepdims=True
    )
    passed = (incoming.astype(jnp.float32) + input_grad).astype(jnp.bfloat16)
    return (passed, hidden_act, gate_grad, up_grad, normed, gain_term)


def local_scatter(section_inputs, gain, w_gate, w_up, w_out, out_grad):
    section_count = lax.axis_size("section")
    position = lax.axis_index("section")
    inputs_here = section_inputs[0]
    gain_row = gain[0]
    w_gate_mat = w_gate[0]
    w_up_mat = w_up[0]
    w_out_mat = w_out[0]
    micro_count, tok_rows, model_width = inputs_here.shape
    hidden_width = w_gate_mat.shape[1]
    token_scale = 1.0 / (micro_count * tok_rows)

    def backward(inputs_row, incoming):
        return section_back(inputs_row, incoming, gain_row, w_gate_mat, w_up_mat, w_out_mat)

    narrow_rows = jnp.zeros((micro_count, tok_rows, model_width), jnp.bfloat16)
    wide_rows = jnp.zeros((micro_count, tok_rows, hidden_width), jnp.bfloat16)
    store = (
        narrow_rows,
        wide_rows,
        wide_rows,
        wide_rows,
        narrow_rows,
        narrow_rows,
        jnp.zeros((model_width,), jnp.float32),
    )

    def run_all(operand):
        incoming_all, previous = operand
        results = [
            backward(inputs_here[member], incoming_all[member]) for member in range(micro_count)
        ]
        gain_sum = results[0][5]
        member = 1
        gain_sum = gain_sum + results[member][5]
        stacked = tuple((jnp.stack([result[index] for result in results]) for index in range(5)))
        return stacked + (incoming_all, gain_sum)

    incoming_all = out_grad
    for section_level in reversed(range(section_count)):
        store = lax.cond(
            position == section_level, run_all, lambda operand: operand[1], (incoming_all, store)
        )
        if section_level > 0:
            incoming_all = from_behind(store[0], "section", -1)
    hidden_flat = store[1].reshape(-1, hidden_width)
    gate_flat = store[2].reshape(-1, hidden_width)
    up_flat = store[3].reshape(-1, hidden_width)
    normed_flat = store[4].reshape(-1, model_width)
    incoming_flat = store[5].reshape(-1, model_width)
    contract = (((0,), (0,)), ((), ()))
    gate_part = lax.dot_general(
        normed_flat, gate_flat, contract, preferred_element_type=jnp.float32
    )
    up_part = lax.dot_general(normed_flat, up_flat, contract, preferred_element_type=jnp.float32)
    out_part = lax.dot_general(
        incoming_flat, hidden_flat, contract, preferred_element_type=jnp.float32
    )
    all_rows = lax.psum_scatter(
        jnp.concatenate([gate_part, up_part, out_part], axis=1) * token_scale,
        "dp",
        scatter_dimension=0,
        tiled=True,
    )
    gate_rows = all_rows[:, :hidden_width]
    up_rows = all_rows[:, hidden_width : 2 * hidden_width]
    out_rows = all_rows[:, 2 * hidden_width :]
    gain_rows = lax.psum_scatter(store[6] * token_scale, "dp", scatter_dimension=0, tiled=True)
    return (gate_rows[None], up_rows[None], out_rows[None], gain_rows[None], store[0][None])


def forward_parts(rows, gain_row, w_gate_mat, w_up_mat):
    rows_float = rows.astype(jnp.float32)
    inverse_rms = lax.rsqrt(jnp.mean(rows_float * rows_float, axis=-1, keepdims=True) + EPSILON)
    normed = (rows_float * inverse_rms * gain_row).astype(jnp.bfloat16)
    gate_pre = jnp.dot(normed, w_gate_mat, preferred_element_type=jnp.float32)
    up_pre = jnp.dot(normed, w_up_mat, preferred_element_type=jnp.float32)
    gelu_value, gelu_slope = gelu_parts(gate_pre)
    hidden_act = (gelu_value * up_pre).astype(jnp.bfloat16)
    gate_factor = (up_pre * gelu_slope).astype(jnp.bfloat16)
    up_factor = gelu_value.astype(jnp.bfloat16)
    return (inverse_rms, normed, hidden_act, gate_factor, up_factor)


def local_gather(section_inputs, gain, w_gate, w_up, w_out, out_grad):
    section_count = lax.axis_size("section")
    position = lax.axis_index("section")
    replica = lax.axis_index("dp")
    replicas = lax.axis_size("dp")
    gain_row = gain[0]
    w_gate_mat = w_gate[0]
    w_up_mat = w_up[0]
    w_out_mat = w_out[0]
    _, micro_count, tok_rows, model_width = section_inputs.shape
    rows_own = micro_count * tok_rows
    token_scale = 1.0 / rows_own
    row_count = model_width // replicas
    rows = section_inputs[0].reshape(rows_own, model_width)
    rows_all = lax.all_gather(rows, "dp", axis=0, tiled=True)
    inverse_rms, _, _, gate_factor, up_factor = forward_parts(rows, gain_row, w_gate_mat, w_up_mat)
    transpose_dims = (((1,), (1,)), ((), ()))

    def stage(operand):
        incoming, _ = operand
        act_grad = jnp.dot(incoming, w_out_mat, preferred_element_type=jnp.float32)
        gate_grad = (act_grad * gate_factor).astype(jnp.bfloat16)
        up_grad = (act_grad * up_factor).astype(jnp.bfloat16)
        normed_grad = lax.dot_general(
            gate_grad, w_gate_mat, transpose_dims, preferred_element_type=jnp.float32
        ) + lax.dot_general(up_grad, w_up_mat, transpose_dims, preferred_element_type=jnp.float32)
        rows_float = rows.astype(jnp.float32)
        gain_term = jnp.sum(normed_grad * rows_float * inverse_rms, axis=0)
        scaled_grad = normed_grad * gain_row
        input_grad = inverse_rms * scaled_grad - rows_float * inverse_rms**3 * jnp.mean(
            scaled_grad * rows_float, axis=-1, keepdims=True
        )
        passed = (incoming.astype(jnp.float32) + input_grad).astype(jnp.bfloat16)
        return (passed, incoming, gain_term)

    incoming = out_grad.reshape(rows_own, model_width)
    store = (
        jnp.zeros((rows_own, model_width), jnp.bfloat16),
        jnp.zeros((rows_own, model_width), jnp.bfloat16),
        jnp.zeros((model_width,), jnp.float32),
    )
    for level in reversed(range(section_count)):
        store = lax.cond(position == level, stage, lambda operand: operand[1], (incoming, store))
        if level > 0:
            incoming = lax.ppermute(store[0], "section", [(level, level - 1)])
    passed, incoming, gain_term = store
    incoming_all = lax.all_gather(incoming, "dp", axis=0, tiled=True)
    gain_all = lax.all_gather(gain_term, "dp", axis=0)
    _, normed_all, hidden_all, gate_factor_all, up_factor_all = forward_parts(
        rows_all, gain_row, w_gate_mat, w_up_mat
    )
    act_all = jnp.dot(incoming_all, w_out_mat, preferred_element_type=jnp.float32)
    gate_all = (act_all * gate_factor_all).astype(jnp.bfloat16)
    up_all = (act_all * up_factor_all).astype(jnp.bfloat16)
    own = replica * row_count
    normed_own = lax.dynamic_slice_in_dim(normed_all, own, row_count, axis=1)
    incoming_own = lax.dynamic_slice_in_dim(incoming_all, own, row_count, axis=1)
    contract = (((0,), (0,)), ((), ()))

    def grad_rows(left, right):
        total = lax.dot_general(left, right, contract, preferred_element_type=jnp.float32)
        return (total * token_scale)[None]

    gain_rows = lax.dynamic_slice_in_dim(gain_all, own, row_count, axis=1).sum(axis=0)
    return (
        grad_rows(normed_own, gate_all),
        grad_rows(normed_own, up_all),
        grad_rows(incoming_own, hidden_all),
        (gain_rows * token_scale)[None],
        passed.reshape(section_inputs.shape),
    )


def local(section_inputs, gain, w_gate, w_up, w_out, out_grad):
    _, micro_count, tok_rows, _ = section_inputs.shape
    gathered_rows = lax.axis_size("dp") * micro_count * tok_rows
    plan = local_gather if 2 * gathered_rows <= 3 * w_gate.shape[2] else local_scatter
    return plan(section_inputs, gain, w_gate, w_up, w_out, out_grad)


def solution(mesh):
    placed = (
        P("section", None, "dp", None),
        P("section", None),
        P("section", None, None),
        P("section", None, None),
        P("section", None, None),
        P(None, "dp", None),
    )
    return jax.shard_map(
        local,
        mesh=mesh,
        in_specs=placed,
        out_specs=(
            P("section", "dp", None),
            P("section", "dp", None),
            P("section", "dp", None),
            P("section", "dp"),
            P("section", None, "dp", None),
        ),
        check_vma=False,
    )
```

profile of v0, /device:TPU:0, one launch (start us, length us, event | category | flops | bytes accessed | tf_op | source)
XLA Modules:
  0.0 210.4 jit_solution(2766487330108355180)
XLA Ops:
  8.0 1.2 fusion.59
  9.2 1.2 fusion.61
  10.4 3.3 %multiply_convert_fusion.34 = (bf16[256,1536]{1,0:T(8,128)(2,1)S(1)}, f32[256,1536]{1,0:T(8,128)S(1)}) fusion(bf16[256,1024]{1,0:T(8,128)(2,1)S(1)} %bitcast.81, bf16[1,1024,1536]{2,1,0:T(8,128)(2,1)} %param.16), kind=kOutput, calls=%fused_computation.101 | convolution fusion | flops 808845312 | bytes 6029312 | tf_op jit(solution)/shard_map/dot_general | solution.py:128
  13.8 1.5 fusion.47
  15.8 1.0 copy-done.6
  16.8 0.9 conditional.4
  19.2 1.3 collective-permute-start.2
  20.5 33.4 %collective-permute-done.2 = bf16[256,1024]{1,0:T(8,128)(2,1)S(1)} collective-permute-done((bf16[256,1024]{1,0:T(8,128)(2,1)}, bf16[256,1024]{1,0:T(8,128)(2,1)S(1)}, u32[]{:S(2)}, u32[]{:S(2)}) %collective-permute-start.2) | collective-permute-done | bytes 524320 | tf_op jit(solution)/shard_map/ppermute | solution.py:181
  53.9 7.5 %conditional.7 = (bf16[256,1024]{1,0:T(8,128)(2,1)S(1)}, f32[1024]{0:T(1024)S(1)}, bf16[1,2,128,1024]{3,2,1,0:T(8,128)(2,1)}) conditional(s32[]{:T(128)} %convert_element_type.144, (bf16[256,1024]{1,0:T(8,128)(2,1)S(1)}, f32[1024]{0:T(1024)S(1)}, bf16[256,1024]{1,0:T(8,128)(2,1)}) %tuple.66, (bf16[256,1024]{1,0:T(8,128)(2,1)S(1)}, ...), branch_computations={%region_14.15_spmd, %region_15.18_spmd} | conditional | flops 2422734336 | bytes 48780368 | solution.py:179
  53.9 3.0 %fusion.93 = f32[256,1536]{1,0:T(8,128)S(1)} fusion(bf16[256,1024]{1,0:T(8,128)(2,1)S(1)} %get-tuple-element.193, bf16[1024,1536]{1,0:T(8,128)(2,1)} %get-tuple-element.125), kind=kOutput, calls=%fused_computation.142 | convolution fusion | flops 805306368 | bytes 5242880 | tf_op jit(solution)/shard_map/cond/branch_1_fun/dot_general | solution.py:157
  56.9 1.0 fusion.31
  58.8 1.3 fusion.30
  60.1 1.2 fusion.29
  62.1 31.4 %all-gather = f32[8192]{0:T(1024)S(1)} all-gather(f32[1024]{0:T(1024)S(1)} %get-tuple-element.152), channel_id=2, replica_groups=mesh['section'=4,'dp'=8] {'dp'}, dimensions={0}, use_global_device_ids=true | all-gather | bytes 36864 | tf_op jit(solution)/shard_map/all_gather | solution.py:184
  94.1 3.5 %fusion.39 = f32[2048]{0:T(1024)S(1)} fusion(bf16[2048,1024]{1,0:T(8,128)(2,1)} %all-gather.4.cloned.1.call-done), kind=kLoop, calls=%fused_computation.79 | loop fusion | flops 6289408 | bytes 4202496 | tf_op jit(solution)/shard_map/reduce_sum | solution.py:126
  98.0 1.1 fusion.41
  99.8 9.3 %fusion.68 = f32[2048,1536]{1,0:T(8,128)} fusion(bf16[2048,1024]{1,0:T(8,128)(2,1)S(1)} %fusion.41, bf16[1,1024,1536]{2,1,0:T(8,128)(2,1)S(1)} %copy-done.2), kind=kOutput, calls=%fused_computation.117 | convolution fusion | flops 6442450944 | bytes 19922944 | tf_op jit(solution)/shard_map/dot_general | solution.py:128
  109.1 9.4 %fusion.72 = f32[2048,1536]{1,0:T(8,128)} fusion(bf16[2048,1024]{1,0:T(8,128)(2,1)S(1)} %fusion.41, bf16[1,1024,1536]{2,1,0:T(8,128)(2,1)S(1)} %copy-done.8), kind=kOutput, calls=%fused_computation.121 | convolution fusion | flops 6442450944 | bytes 19922944 | tf_op jit(solution)/shard_map/dot_general | solution.py:129
  118.5 41.6 %all-gather.6.cloned.1.call-done = bf16[2048,1024]{1,0:T(8,128)(2,1)} async-done(((bf16[256,1024]{1,0:T(8,128)(2,1)}), bf16[2048,1024]{1,0:T(8,128)(2,1)}) %all-gather.6.cloned.1.call-update) | async-done | bytes 4194320 | tf_op jit(solution)/shard_map/all_gather | solution.py:183
  160.1 9.5 %fusion.75 = f32[2048,1536]{1,0:T(8,128)S(1)} fusion(bf16[2048,1024]{1,0:T(8,128)(2,1)} %all-gather.6.cloned.1.call-done, bf16[1,1024,1536]{2,1,0:T(8,128)(2,1)} %param.18), kind=kOutput, calls=%fused_computation.124 | convolution fusion | flops 6442450944 | bytes 19922944 | tf_op jit(solution)/shard_map/dot_general | solution.py:188
  169.6 4.5 %copy-done.18 = f32[2048,1536]{1,0:T(8,128)} copy-done((f32[2048,1536]{1,0:T(8,128)}, f32[2048,1536]{1,0:T(8,128)S(1)}, u32[]{:S(2)}) %copy-start.18) | copy-done | bytes 12582936
  174.1 7.2 %fusion.51 = f32[1,128,1536]{2,1,0:T(8,128)} fusion(f32[2048,1536]{1,0:T(8,128)S(1)} %fusion.75, f32[2048,1536]{1,0:T(8,128)S(1)} %copy-done.17, bf16[2048,1024]{1,0:T(8,128)(2,1)} %copy-done.15, s32[]{:T(128)S(6)} %select_n.2), kind=kOutput, calls=%fused_computation.91 | convolution fusion | flops 843251712 | bytes 26476548 | tf_op jit(solution)/shard_map/dot_general | solution.py:197
  181.3 13.8 %fusion.53 = f32[1,128,1536]{2,1,0:T(8,128)} fusion(f32[2048,1536]{1,0:T(8,128)} %copy-done.18, f32[2048,1536]{1,0:T(8,128)} %fusion.72, f32[2048,1536]{1,0:T(8,128)S(1)} %copy-done.17, bf16[2048,1024]{1,0:T(8,128)(2,1)} %copy-done.15, s32[]{:T(128)S(6)} %select_n.2), kind=kOutput, calls=%fused_computation.93 | convolution fusion | flops 874708992 | bytes 39059460 | tf_op jit(solution)/shard_map/dot_general | solution.py:197
  195.0 8.6 %fusion.49 = f32[1,128,1536]{2,1,0:T(8,128)} fusion(f32[2048,1536]{1,0:T(8,128)} %fusion.72, f32[2048,1536]{1,0:T(8,128)S(1)} %copy-done.17, bf16[2048,1024]{1,0:T(8,128)(2,1)} %all-gather.6.cloned.1.call-done, s32[]{:T(128)S(6)} %select_n.2), kind=kOutput, calls=%fused_computation.89 | convolution fusion | flops 836960256 | bytes 26476548 | tf_op jit(solution)/shard_map/dot_general | solution.py:197
  (50 shorter events, 7.0 us)
Async XLA Ops:
  7.2 86.9 %all-gather.4.cloned.1.call-start = ((), (), s32[]{:S(2)}) async-start(), calls=%async_computation | async-start | bytes 4718592 | tf_op jit(solution)/shard_map/all_gather | solution.py:151
  7.9 152.2 %all-gather.6.cloned.1.call-start = ((), (), s32[]{:S(2)}) async-start(), calls=%async_computation.1 | async-start | bytes 4718592 | tf_op jit(solution)/shard_map/all_gather | solution.py:183
  10.4 3.3 %copy-start.7 = (bf16[1,1024,1536]{2,1,0:T(8,128)(2,1)S(1)}, bf16[1,1024,1536]{2,1,0:T(8,128)(2,1)}, u32[]{:S(2)}) copy-start(bf16[1,1024,1536]{2,1,0:T(8,128)(2,1)} %param.17) | copy-start | bytes 9437188
  13.7 1.6 copy-start
  13.7 2.1 copy-start.1
  13.8 3.0 %copy-start.6 = (bf16[1,1024,1536]{2,1,0:T(8,128)(2,1)S(1)}, bf16[1,1024,1536]{2,1,0:T(8,128)(2,1)}, u32[]{:S(2)}) copy-start(bf16[1,1024,1536]{2,1,0:T(8,128)(2,1)} %param.18) | copy-start | bytes 9437188
  13.8 3.0 %copy-start.14 = (bf16[2,128,1024]{2,1,0:T(8,128)(2,1)S(1)}, bf16[2,128,1024]{2,1,0:T(8,128)(2,1)}, u32[]{:S(2)}) copy-start(bf16[2,128,1024]{2,1,0:T(8,128)(2,1)} %param.19) | copy-start | bytes 1572868
  13.8 3.0 %copy-start.16 = (f32[1,1024]{1,0:T(1,128)S(1)}, f32[1,1024]{1,0:T(1,128)}, u32[]{:S(2)}) copy-start(f32[1,1024]{1,0:T(1,128)} %param.15) | copy-start | bytes 12292
  17.7 0.7 collective-permute-start
  18.4 0.7 collective-permute-start.1
  19.2 34.7 %collective-permute-start.2 = (bf16[256,1024]{1,0:T(8,128)(2,1)}, bf16[256,1024]{1,0:T(8,128)(2,1)S(1)}, u32[]{:S(2)}, u32[]{:S(2)}) collective-permute-start(bf16[256,1024]{1,0:T(8,128)(2,1)} %get-tuple-element.198), channel_id=1, source_target_pairs={{8,0},{9,1},{10,2},{11,3},{12,4},{13,5},{14,6},{15,7}} | collective-permute-start | bytes 1572872 | tf_op jit(solution)/shard_map/ppermute | solution.py:181
  53.9 3.1 %copy-start.5 = (bf16[1024,1536]{1,0:T(8,128)(2,1)S(1)}, bf16[1024,1536]{1,0:T(8,128)(2,1)}, u32[]{:S(2)}) copy-start(bf16[1024,1536]{1,0:T(8,128)(2,1)} %get-tuple-element.127) | copy-start | bytes 9437188 | tf_op jit(solution)/shard_map/cond
  56.9 1.9 copy-start.11
  61.3 0.8 copy-start.13
  94.1 3.9 %copy-start.12 = (bf16[2048,1024]{1,0:T(8,128)(2,1)S(1)}, bf16[2048,1024]{1,0:T(8,128)(2,1)}, u32[]{:S(2)}) copy-start(bf16[2048,1024]{1,0:T(8,128)(2,1)} %all-gather.4.cloned.1.call-done) | copy-start | bytes 12582916
  98.0 1.9 copy-start.2
  99.8 9.3 %copy-start.15 = (bf16[2048,1024]{1,0:T(8,128)(2,1)}, bf16[2048,1024]{1,0:T(8,128)(2,1)S(1)}, u32[]{:S(2)}) copy-start(bf16[2048,1024]{1,0:T(8,128)(2,1)S(1)} %fusion.41) | copy-start | bytes 12582916
  99.8 9.3 %copy-start.8 = (bf16[1,1024,1536]{2,1,0:T(8,128)(2,1)S(1)}, bf16[1,1024,1536]{2,1,0:T(8,128)(2,1)}, u32[]{:S(2)}) copy-start(bf16[1,1024,1536]{2,1,0:T(8,128)(2,1)} %param.17) | copy-start | bytes 9437188
  160.1 14.0 %copy-start.17 = (f32[2048,1536]{1,0:T(8,128)S(1)}, f32[2048,1536]{1,0:T(8,128)}, u32[]{:S(2)}) copy-start(f32[2048,1536]{1,0:T(8,128)} %fusion.68) | copy-start | bytes 37748740
  169.6 4.5 %copy-start.18 = (f32[2048,1536]{1,0:T(8,128)}, f32[2048,1536]{1,0:T(8,128)S(1)}, u32[]{:S(2)}) copy-start(f32[2048,1536]{1,0:T(8,128)S(1)} %fusion.75) | copy-start | bytes 37748740
Sparse Core Ops, SparseCore 0:
  10.1 75.9 all-gather.3
  88.8 71.2 all-gather.5
where the time goes:
time: 211 us; the launch traced here: 210 us
  waiting for transfers between devices  75.7 us (36%)
  matrix products  67.8 us (32%)
  blocking collectives  31.4 us (15%)
  between operations  14.3 us (7%)
  local copies, waits for them, and re-layouts  9.73 us (5%)
  other arithmetic  8.75 us (4%)
  starting transfers between devices  2.74 us (1%)
    all_gather x1, waiting for transfers between devices, local_gather(): incoming_all = lax.all_gather(incoming, 'dp', axis=0, tiled=True)  41.6 us
    ppermute x3, waiting for transfers between devices, local_gather(): incoming = lax.ppermute(store[0], 'section', [(level, level - 1)])  33.4 us
    all_gather x1, blocking collectives, local_gather(): gain_all = lax.all_gather(gain_term, 'dp', axis=0)  31.4 us
    dot_general x3, matrix products, grad_rows(): lax.dot_general(left, right, contract, preferred_element_type=jnp.float32)  29.5 us
    dot_general x2, matrix products, forward_parts(): gate_pre = jnp.dot(normed, w_gate_mat, preferred_element_type=jnp.float32)  12.5 us
    dot_general x2, matrix products, forward_parts(): up_pre = jnp.dot(normed, w_up_mat, preferred_element_type=jnp.float32)  10.9 us
    dot_general x1, matrix products, local_gather(): jnp.dot(incoming_all, w_out_mat, preferred_element_type=jnp.float32)  9.5 us
    unnamed x26, local copies, waits for them, and re-layouts  7.93 us
  transfers between devices with their start and end apart: 5, of which 2 were waited for; matrix products, arithmetic and copies ran while one was open for 18% of the time, Pallas kernels for 0%

commit v1 on v0

--- a/solution.py
+++ b/solution.py
@@ -148,7 +148,6 @@
     token_scale = 1.0 / rows_own
     row_count = model_width // replicas
     rows = section_inputs[0].reshape(rows_own, model_width)
-    rows_all = lax.all_gather(rows, "dp", axis=0, tiled=True)
     inverse_rms, _, _, gate_factor, up_factor = forward_parts(rows, gain_row, w_gate_mat, w_up_mat)
     transpose_dims = (((1,), (1,)), ((), ()))
 
@@ -180,7 +179,11 @@
         if level > 0:
             incoming = lax.ppermute(store[0], "section", [(level, level - 1)])
     passed, incoming, gain_term = store
-    incoming_all = lax.all_gather(incoming, "dp", axis=0, tiled=True)
+    rows_all, incoming_all = jnp.split(
+        lax.all_gather(jnp.concatenate([rows, incoming], axis=1), "dp", axis=0, tiled=True),
+        [rows.shape[1]],
+        axis=1,
+    )
     gain_all = lax.all_gather(gain_term, "dp", axis=0)
     _, normed_all, hidden_all, gate_factor_all, up_factor_all = forward_parts(
         rows_all, gain_row, w_gate_mat, w_up_mat

time: 211 us -> 265 us (1.26)
  waiting for transfers between devices: 75.7 us -> 125 us
  matrix products: 67.8 us -> 73.7 us
  local copies, waits for them, and re-layouts: 9.73 us -> 5.71 us
    all_gather x2 -> x1, waiting for transfers between devices: 41.6 us -> 92.5 us  [local_gather(): lax.all_gather(jnp.concatenate([rows, incoming], axis=1), 'dp', axis=0, t...]
    dot_general x3, matrix products: 29.5 us -> 36.1 us  [grad_rows(): lax.dot_general(left, right, contract, preferred_element_type=jnp.float32)]
    unnamed x26 -> x28, local copies, waits for them, and re-layouts: 7.93 us -> 1.74 us
  transfers between devices with their start and end apart: 5 -> 4, of which waited for: 2 -> 2; matrix products, arithmetic and copies ran while one was open for 18% -> 0% of each run, Pallas kernels for 0% -> 0%
where the time goes in v1:
time: 265 us
  waiting for transfers between devices  125 us (47%)
  matrix products  73.7 us (28%)
  blocking collectives  31.9 us (12%)
  between operations  14.3 us (5%)
  other arithmetic  11.3 us (4%)
  local copies, waits for them, and re-layouts  5.71 us (2%)
  starting transfers between devices  2.71 us (1%)
    all_gather x1, waiting for transfers between devices, local_gather(): lax.all_gather(jnp.concatenate([rows, incoming], axis=1), 'dp', axis=0, t...  92.5 us
    dot_general x3, matrix products, grad_rows(): lax.dot_general(left, right, contract, preferred_element_type=jnp.float32)  36.1 us
    ppermute x3, waiting for transfers between devices, local_gather(): incoming = lax.ppermute(store[0], 'section', [(level, level - 1)])  32.8 us
    all_gather x1, blocking collectives, local_gather(): gain_all = lax.all_gather(gain_term, 'dp', axis=0)  31.9 us
    dot_general x2, matrix products, forward_parts(): gate_pre = jnp.dot(normed, w_gate_mat, preferred_element_type=jnp.float32)  12.6 us
    dot_general x2, matrix products, forward_parts(): up_pre = jnp.dot(normed, w_up_mat, preferred_element_type=jnp.float32)  10.7 us
    dot_general x1, matrix products, local_gather(): jnp.dot(incoming_all, w_out_mat, preferred_element_type=jnp.float32)  9.07 us
  transfers between devices with their start and end apart: 4, of which 2 were waited for; matrix products, arithmetic and copies ran while one was open for 0% of the time, Pallas kernels for 0%

profile of v1, /device:TPU:0, one launch (start us, length us, event | category | flops | bytes accessed | tf_op | source)
XLA Modules:
  0.0 265.0 jit_solution(11230527251541639790)
XLA Ops:
  7.2 1.2 fusion.59
  8.5 1.2 fusion.61
  9.7 3.3 %multiply_convert_fusion.34 = (bf16[256,1536]{1,0:T(8,128)(2,1)S(1)}, f32[256,1536]{1,0:T(8,128)S(1)}) fusion(bf16[256,1024]{1,0:T(8,128)(2,1)S(1)} %bitcast.82, bf16[1,1024,1536]{2,1,0:T(8,128)(2,1)} %param.16), kind=kOutput, calls=%fused_computation.101 | convolution fusion | flops 808845312 | bytes 6029312 | tf_op jit(solution)/shard_map/dot_general | solution.py:128
  13.1 1.5 fusion.47
  15.1 1.0 copy-done.6
  18.4 1.3 collective-permute-start.2
  19.7 32.8 %collective-permute-done.2 = bf16[256,1024]{1,0:T(8,128)(2,1)S(1)} collective-permute-done((bf16[256,1024]{1,0:T(8,128)(2,1)}, bf16[256,1024]{1,0:T(8,128)(2,1)S(1)}, u32[]{:S(2)}, u32[]{:S(2)}) %collective-permute-start.2) | collective-permute-done | bytes 524320 | tf_op jit(solution)/shard_map/ppermute | solution.py:180
  52.6 7.5 %conditional.7 = (bf16[256,1024]{1,0:T(8,128)(2,1)S(1)}, f32[1024]{0:T(1024)S(1)}, bf16[1,2,128,1024]{3,2,1,0:T(8,128)(2,1)}) conditional(s32[]{:T(128)} %convert_element_type.142, (bf16[256,1024]{1,0:T(8,128)(2,1)S(1)}, f32[1024]{0:T(1024)S(1)}, bf16[256,1024]{1,0:T(8,128)(2,1)}) %tuple.66, (bf16[256,1024]{1,0:T(8,128)(2,1)S(1)}, ...), branch_computations={%region_13.0_spmd, %region_14.0_spmd} | conditional | flops 2422734336 | bytes 48780368 | solution.py:178
  52.6 3.0 %fusion.94 = f32[256,1536]{1,0:T(8,128)S(1)} fusion(bf16[256,1024]{1,0:T(8,128)(2,1)S(1)} %get-tuple-element.193, bf16[1024,1536]{1,0:T(8,128)(2,1)} %get-tuple-element.125), kind=kOutput, calls=%fused_computation.144 | convolution fusion | flops 805306368 | bytes 5242880 | tf_op jit(solution)/shard_map/cond/branch_1_fun/dot_general | solution.py:156
  55.6 1.1 fusion.31
  57.5 1.3 fusion.30
  58.8 1.2 fusion.29
  60.0 1.1 pad_maximum_fusion
  61.1 31.9 %all-gather = f32[8192]{0:T(1024)S(1)} all-gather(f32[1024]{0:T(1024)S(1)} %get-tuple-element.152), channel_id=2, replica_groups=mesh['section'=4,'dp'=8] {'dp'}, dimensions={0}, use_global_device_ids=true | all-gather | bytes 36864 | tf_op jit(solution)/shard_map/all_gather | solution.py:187
  93.6 92.5 %all-gather.3.cloned.1.call-done = bf16[2048,2048]{1,0:T(8,128)(2,1)} async-done(((bf16[256,2048]{1,0:T(8,128)(2,1)}), bf16[2048,2048]{1,0:T(8,128)(2,1)}) %all-gather.3.cloned.1.call-update) | async-done | bytes 8388624 | tf_op jit(solution)/shard_map/all_gather | solution.py:183
  186.0 3.1 %fusion.39 = f32[2048]{0:T(1024)S(1)} fusion(bf16[2048,2048]{1,0:T(8,128)(2,1)} %all-gather.3.cloned.1.call-done), kind=kLoop, calls=%fused_computation.79 | loop fusion | flops 6289408 | bytes 4202496 | tf_op jit(solution)/shard_map/reduce_sum | solution.py:126
  189.1 2.9 %fusion.41 = bf16[2048,1024]{1,0:T(8,128)(2,1)S(1)} fusion(f32[1024]{0:T(1024)S(1)} %bitcast.85, f32[2048]{0:T(1024)S(1)} %add_rsqrt_fusion, bf16[2048,2048]{1,0:T(8,128)(2,1)} %all-gather.3.cloned.1.call-done), kind=kLoop, calls=%fused_computation.81 | loop fusion | flops 8388608 | bytes 8400896 | tf_op jit(solution)/shard_map/convert_element_type | solution.py:127
  192.3 9.3 %fusion.68 = f32[2048,1536]{1,0:T(8,128)} fusion(bf16[2048,1024]{1,0:T(8,128)(2,1)S(1)} %fusion.41, bf16[1,1024,1536]{2,1,0:T(8,128)(2,1)S(1)} %copy-done.2), kind=kOutput, calls=%fused_computation.118 | convolution fusion | flops 6442450944 | bytes 19922944 | tf_op jit(solution)/shard_map/dot_general | solution.py:128
  201.6 9.2 %fusion.72 = f32[2048,1536]{1,0:T(8,128)} fusion(bf16[2048,1024]{1,0:T(8,128)(2,1)S(1)} %fusion.41, bf16[1,1024,1536]{2,1,0:T(8,128)(2,1)S(1)} %copy-done.9), kind=kOutput, calls=%fused_computation.122 | convolution fusion | flops 6442450944 | bytes 19922944 | tf_op jit(solution)/shard_map/dot_general | solution.py:129
  210.8 9.1 %fusion.75 = f32[2048,1536]{1,0:T(8,128)} fusion(bf16[1,1024,1536]{2,1,0:T(8,128)(2,1)S(1)} %copy-done.7, bf16[2048,2048]{1,0:T(8,128)(2,1)S(1)} %bitcast.80), kind=kOutput, calls=%fused_computation.125 | convolution fusion | flops 6442450944 | bytes 19922944 | tf_op jit(solution)/shard_map/dot_general | solution.py:191
  219.9 8.5 %fusion.51 = f32[1,128,1536]{2,1,0:T(8,128)} fusion(f32[2048,1536]{1,0:T(8,128)} %fusion.75, f32[2048,1536]{1,0:T(8,128)S(1)} %bitcast.111, bf16[2048,1024]{1,0:T(8,128)(2,1)S(1)} %fusion.41, s32[]{:T(128)S(6)} %select_n.2), kind=kOutput, calls=%fused_computation.91 | convolution fusion | flops 843251712 | bytes 26476548 | tf_op jit(solution)/shard_map/dot_general | solution.py:200
  228.4 16.0 %fusion.53 = f32[1,128,1536]{2,1,0:T(8,128)} fusion(f32[2048,1536]{1,0:T(8,128)} %fusion.75, f32[2048,1536]{1,0:T(8,128)} %fusion.72, f32[2048,1536]{1,0:T(8,128)} %fusion.68, bf16[2048,1024]{1,0:T(8,128)(2,1)S(1)} %fusion.41, s32[]{:T(128)S(6)} %select_n.2), kind=kOutput, calls=%fused_computation.93 | convolution fusion | flops 874708992 | bytes 39059460 | tf_op jit(solution)/shard_map/dot_general | solution.py:200
  244.3 2.2 slice-done.2
  246.5 11.6 %fusion.49 = f32[1,128,1536]{2,1,0:T(8,128)} fusion(f32[2048,1536]{1,0:T(8,128)} %fusion.72, f32[2048,1536]{1,0:T(8,128)} %fusion.68, bf16[2048,1024]{1,0:T(8,128)(2,1)S(1)} %slice-done.2, s32[]{:T(128)S(6)} %select_n.2), kind=kOutput, calls=%fused_computation.89 | convolution fusion | flops 836960256 | bytes 26476548 | tf_op jit(solution)/shard_map/dot_general | solution.py:200
  (54 shorter events, 5.5 us)
Async XLA Ops:
  7.2 178.9 %all-gather.3.cloned.1.call-start = ((), (), s32[]{:S(2)}) async-start(), calls=%async_computation | async-start | bytes 9437184 | tf_op jit(solution)/shard_map/all_gather | solution.py:183
  9.7 3.3 %copy-start.8 = (bf16[1,1024,1536]{2,1,0:T(8,128)(2,1)S(1)}, bf16[1,1024,1536]{2,1,0:T(8,128)(2,1)}, u32[]{:S(2)}) copy-start(bf16[1,1024,1536]{2,1,0:T(8,128)(2,1)} %param.17) | copy-start | bytes 9437188
  13.0 1.6 copy-start
  13.0 2.1 copy-start.1
  13.0 3.0 %copy-start.6 = (bf16[1,1024,1536]{2,1,0:T(8,128)(2,1)S(1)}, bf16[1,1024,1536]{2,1,0:T(8,128)(2,1)}, u32[]{:S(2)}) copy-start(bf16[1,1024,1536]{2,1,0:T(8,128)(2,1)} %param.18) | copy-start | bytes 9437188
  13.0 3.0 %copy-start.13 = (bf16[2,128,1024]{2,1,0:T(8,128)(2,1)S(1)}, bf16[2,128,1024]{2,1,0:T(8,128)(2,1)}, u32[]{:S(2)}) copy-start(bf16[2,128,1024]{2,1,0:T(8,128)(2,1)} %param.19) | copy-start | bytes 1572868
  13.0 3.0 %copy-start.14 = (f32[1,1024]{1,0:T(1,128)S(1)}, f32[1,1024]{1,0:T(1,128)}, u32[]{:S(2)}) copy-start(f32[1,1024]{1,0:T(1,128)} %param.15) | copy-start | bytes 12292
  17.0 0.7 collective-permute-start
  17.7 0.7 collective-permute-start.1
  18.4 34.1 %collective-permute-start.2 = (bf16[256,1024]{1,0:T(8,128)(2,1)}, bf16[256,1024]{1,0:T(8,128)(2,1)S(1)}, u32[]{:S(2)}, u32[]{:S(2)}) collective-permute-start(bf16[256,1024]{1,0:T(8,128)(2,1)} %get-tuple-element.198), channel_id=1, source_target_pairs={{8,0},{9,1},{10,2},{11,3},{12,4},{13,5},{14,6},{15,7}} | collective-permute-start | bytes 1572872 | tf_op jit(solution)/shard_map/ppermute | solution.py:180
  52.6 3.1 %copy-start.5 = (bf16[1024,1536]{1,0:T(8,128)(2,1)S(1)}, bf16[1024,1536]{1,0:T(8,128)(2,1)}, u32[]{:S(2)}) copy-start(bf16[1024,1536]{1,0:T(8,128)(2,1)} %get-tuple-element.127) | copy-start | bytes 9437188 | tf_op jit(solution)/shard_map/cond
  55.6 1.9 copy-start.12
  189.1 3.2 %copy-start.2 = (bf16[1,1024,1536]{2,1,0:T(8,128)(2,1)S(1)}, bf16[1,1024,1536]{2,1,0:T(8,128)(2,1)}, u32[]{:S(2)}) copy-start(bf16[1,1024,1536]{2,1,0:T(8,128)(2,1)} %param.16) | copy-start | bytes 9437188
  192.3 9.3 %copy-start.9 = (bf16[1,1024,1536]{2,1,0:T(8,128)(2,1)S(1)}, bf16[1,1024,1536]{2,1,0:T(8,128)(2,1)}, u32[]{:S(2)}) copy-start(bf16[1,1024,1536]{2,1,0:T(8,128)(2,1)} %param.17) | copy-start | bytes 9437188
  192.3 18.5 %slice-start = ((s8[8388608]{0:T(1024)(128)(4,1)}), s8[4194304]{0:T(1024)(128)(4,1)S(1)}, s32[]{:S(2)}) async-start(s8[8388608]{0:T(1024)(128)(4,1)} %bitcast.79), calls=%async_computation.1 | async-start | bytes 8388608
  201.6 9.2 %copy-start.7 = (bf16[1,1024,1536]{2,1,0:T(8,128)(2,1)S(1)}, bf16[1,1024,1536]{2,1,0:T(8,128)(2,1)}, u32[]{:S(2)}) copy-start(bf16[1,1024,1536]{2,1,0:T(8,128)(2,1)} %param.18) | copy-start | bytes 9437188
  201.6 9.2 %slice-start.1 = ((s8[8388608]{0:T(1024)(128)(4,1)}), s8[4194304]{0:T(1024)(128)(4,1)S(1)}, s32[]{:S(2)}) async-start(s8[8388608]{0:T(1024)(128)(4,1)} %bitcast.79), calls=%async_computation.2 | async-start | bytes 8388608
  201.6 18.3 %slice-start.3 = ((s8[12582912]{0:T(1024)(128)(4,1)}), s8[4194304]{0:T(1024)(128)(4,1)S(1)}, s32[]{:S(2)}) async-start(s8[12582912]{0:T(1024)(128)(4,1)} %bitcast.110), calls=%async_computation.4 | async-start | bytes 8388608
  201.6 18.3 %slice-start.4 = ((s8[12582912]{0:T(1024)(128)(4,1)}), s8[4194304]{0:T(1024)(128)(4,1)S(1)}, s32[]{:S(2)}) async-start(s8[12582912]{0:T(1024)(128)(4,1)} %bitcast.110), calls=%async_computation.5 | async-start | bytes 8388608
  210.8 9.1 %slice-start.5 = ((s8[12582912]{0:T(1024)(128)(4,1)}), s8[4194304]{0:T(1024)(128)(4,1)S(1)}, s32[]{:S(2)}) async-start(s8[12582912]{0:T(1024)(128)(4,1)} %bitcast.110), calls=%async_computation.6 | async-start | bytes 8388608
  244.3 2.2 slice-start.2
Sparse Core Ops, SparseCore 0:
  61.2 124.7 all-gather.2
